TPU v7x, 32 devices: a whole 2x2x4 slice. The times are simulated.
32 devices in a mesh: ep: 8 (over y, x, core), tp: 4 (over z).
Axes of the slice: x: 2, y: 2, z: 4, core: 2. Of those that a mesh axis runs over, the one named last changes fastest.
Arguments:
- tokens: bfloat16 [5120, 2048], P('ep'), may hold values from -6 to 6
- norm1_gain: float32 [2048], replicated, may hold values from 0.1 to 1.9
- w_qkv: bfloat16 [3, 2048, 2048], P(None, None, 'tp'), may hold values from -0.125 to 0.125
- b_qkv: bfloat16 [3, 16, 128], P(None, 'tp'), may hold values from -3 to 3
- w_out: bfloat16 [2048, 2048], P('tp'), may hold values from -1.25 to 1.25
- norm2_gain: float32 [2048], replicated, may hold values from 0.1 to 1.9
- w_router: bfloat16 [2048, 8], replicated, may hold values from -0.0625 to 0.0625
- w_sgate: bfloat16 [2048], replicated, may hold values from -0.125 to 0.125
- w_shared_gu: bfloat16 [2, 2048, 5632], P(None, None, 'tp'), may hold values from -0.125 to 0.125
- w_shared_down: bfloat16 [5632, 2048], P('tp'), may hold values from -0.15625 to 0.15625
- w_expert_gu: bfloat16 [8, 2, 2048, 1408], P('ep', None, None, 'tp'), may hold values from -0.125 to 0.125
- w_expert_down: bfloat16 [8, 1408, 2048], P('ep', 'tp'), may hold values from -0.3125 to 0.3125
- routes: int32 [5120, 4], P('ep'), may hold values from 0 to 7, all different within a row; in each aligned block of 640 rows (0 to 639, 640 to 1279, ...) at most 400 rows name the same one
- grad_out: bfloat16 [5120, 2048], P('ep'), may hold values from -6 to 6
Outputs:
- output: bfloat16 [5120, 2048], P(('ep', 'tp'))
- grad_tokens: float32 [5120, 2048], P(('ep', 'tp'))
- grad_norm1_gain: float32 [2048], P('ep')
- grad_w_qkv: float32 [3, 2048, 2048], P(None, 'ep', 'tp')
- grad_b_qkv: float32 [3, 16, 128], P(None, 'tp', 'ep')
- grad_w_out: float32 [2048, 2048], P('tp', 'ep')
- grad_norm2_gain: float32 [2048], P('ep')
- grad_w_router: float32 [2048, 8], P('ep')
- grad_w_sgate: float32 [2048], P('ep')
- grad_w_shared_gu: float32 [2, 2048, 5632], P(None, 'ep', 'tp')
- grad_w_shared_down: float32 [5632, 2048], P('tp', 'ep')
- grad_w_expert_gu: float32 [8, 2, 2048, 1408], P('ep', None, None, 'tp')
- grad_w_expert_down: float32 [8, 1408, 2048], P('ep', 'tp')
Inputs may be any that keep to these rules, and one draw needn't show every extreme that they name: `routes`: each row names 4 different experts. Among the rows of one sequence no expert is named more than 400 times, and in every draw some expert is named exactly 400 times within some sequence.
All inputs are finite; a program needn't handle non-finite values.
Results may differ from a plain program's by a relative error of at most 0.024.
Values may be sent and summed in bfloat16 or wider, within the bound.
A program may use at most 384 MiB of HBM per device.

v0:
```python
import jax
import jax.numpy as jnp
from jax import lax
from jax.sharding import PartitionSpec as P

norm_eps = 1e-06
rope_base = 1000000.0
masked_score = -1e30


def contract(left_side, right_side, left_dim, right_dim):
    return lax.dot_general(
        left_side,
        right_side,
        (((left_dim,), (right_dim,)), ((), ())),
        preferred_element_type=jnp.float32,
    )


def rms_forward(hidden, gain_vector):
    inv_scale = lax.rsqrt(jnp.mean(hidden * hidden, axis=-1, keepdims=True) + norm_eps)
    normed = hidden * inv_scale
    return (normed * gain_vector, normed, inv_scale)


def rms_backward(grad_normed_out, gain_vector, normed, inv_scale):
    grad_scaled = grad_normed_out * gain_vector
    grad_gain = jnp.sum(grad_normed_out * normed, axis=0)
    inner_mean = jnp.mean(grad_scaled * normed, axis=-1, keepdims=True)
    return (inv_scale * (grad_scaled - normed * inner_mean), grad_gain)


def rope_tables(length, head_dim):
    half_dim = head_dim // 2
    frequency = rope_base ** (-(jnp.arange(half_dim, dtype=jnp.float32) * 2.0) / head_dim)
    angles = jnp.arange(length, dtype=jnp.float32)[:, None] * frequency[None, :]
    cosine_table = jnp.concatenate([jnp.cos(angles), jnp.cos(angles)], axis=-1)[:, None, :]
    sine_table = jnp.concatenate([jnp.sin(angles), jnp.sin(angles)], axis=-1)[:, None, :]
    return (cosine_table, sine_table)


def rotate_forward(values, cosine_table, sine_table):
    half_dim = values.shape[-1] // 2
    turned = jnp.concatenate([-values[..., half_dim:], values[..., :half_dim]], axis=-1)
    return values * cosine_table + turned * sine_table


def rotate_backward(grad_rows, cosine_table, sine_table):
    half_dim = grad_rows.shape[-1] // 2
    scaled = grad_rows * sine_table
    turned = jnp.concatenate([scaled[..., half_dim:], -scaled[..., :half_dim]], axis=-1)
    return grad_rows * cosine_table + turned


def gated_backward(grad_act, gate_up):
    sigmoid_gate = jax.nn.sigmoid(gate_up[0])
    grad_gate = grad_act * gate_up[1] * sigmoid_gate * (1.0 + gate_up[0] * (1.0 - sigmoid_gate))
    grad_up = grad_act * gate_up[0] * sigmoid_gate
    return jnp.stack([grad_gate, grad_up]).astype(jnp.bfloat16)


def slot_table(routes, experts, capacity):
    pair_experts = routes.reshape(-1)
    choose = (pair_experts[:, None] == jnp.arange(experts, dtype=jnp.int32)[None, :]).astype(
        jnp.int32
    )
    before = jnp.cumsum(choose, axis=0) - choose
    slot_number = jnp.sum(before * choose, axis=1)
    slot_dest = pair_experts * capacity + slot_number
    pair_count = pair_experts.shape[0]
    slot_owner = (
        jnp.full((experts * capacity,), pair_count, jnp.int32)
        .at[slot_dest]
        .set(jnp.arange(pair_count, dtype=jnp.int32))
    )
    return (slot_dest, slot_owner)


def per_device(
    tokens,
    norm1_gain,
    w_qkv,
    b_qkv,
    w_out,
    norm2_gain,
    w_router,
    w_sgate,
    w_shared_gu,
    w_shared_down,
    w_expert_gu,
    w_expert_down,
    routes,
    grad_out,
):
    seq_rows, features = tokens.shape
    top_count = routes.shape[1]
    expert_count = w_router.shape[1]
    heads_here = b_qkv.shape[1]
    head_dim = b_qkv.shape[2]
    lane_count = lax.axis_size("tp")
    lane_index = lax.axis_index("tp")
    capacity = lane_count * (5 * seq_rows * top_count // (4 * expert_count * lane_count))
    out_rows = seq_rows // lane_count
    row_start = lane_index * out_rows
    score_scale = head_dim ** (-0.5)
    residual = tokens.astype(jnp.float32)
    normed_one, unit_one, scale_one = rms_forward(residual, norm1_gain)
    low_one = normed_one.astype(jnp.bfloat16)
    qkv_pre = jnp.einsum("ld,cde->cle", low_one, w_qkv, preferred_element_type=jnp.float32)
    qkv_pre = qkv_pre + b_qkv.reshape(3, 1, -1).astype(jnp.float32)
    cosine_table, sine_table = rope_tables(seq_rows, head_dim)
    shaped = qkv_pre.reshape(3, seq_rows, heads_here, head_dim)
    queries = rotate_forward(shaped[0], cosine_table, sine_table).astype(jnp.bfloat16)
    key_rows = rotate_forward(shaped[1], cosine_table, sine_table).astype(jnp.bfloat16)
    value_rows = shaped[2].astype(jnp.bfloat16)
    positions = jnp.arange(seq_rows)
    causal = positions[None, :] <= positions[:, None]

    def attn_scores():
        raw_scores = (
            jnp.einsum("qhd,khd->hqk", queries, key_rows, preferred_element_type=jnp.float32)
            * score_scale
        )
        return jnp.where(causal[None], raw_scores, masked_score)

    scores = attn_scores()
    score_peak = jnp.max(scores, axis=-1, keepdims=True)
    log_total = score_peak + jnp.log(jnp.sum(jnp.exp(scores - score_peak), axis=-1, keepdims=True))
    attn_probs = jnp.exp(scores - log_total).astype(jnp.bfloat16)
    attn_mixed = jnp.einsum(
        "hqk,khd->qhd", attn_probs, value_rows, preferred_element_type=jnp.float32
    )
    attn_mixed = attn_mixed.reshape(seq_rows, -1).astype(jnp.bfloat16)
    attn_total = lax.psum(jnp.dot(attn_mixed, w_out, preferred_element_type=jnp.float32), "tp")
    hidden = residual + attn_total
    normed_two, unit_two, scale_two = rms_forward(hidden, norm2_gain)
    low_two = normed_two.astype(jnp.bfloat16)
    router_probs = jax.nn.softmax(
        jnp.dot(low_two, w_router, preferred_element_type=jnp.float32), axis=-1
    )
    route_hits = (
        routes[:, :, None] == jnp.arange(expert_count, dtype=jnp.int32)[None, None, :]
    ).astype(jnp.float32)
    gate_values = jnp.sum(router_probs[:, None, :] * route_hits, axis=-1)
    shared_gate = jax.nn.sigmoid(jnp.dot(low_two, w_sgate, preferred_element_type=jnp.float32))
    shared_gu = jnp.einsum("ld,cdf->clf", low_two, w_shared_gu, preferred_element_type=jnp.float32)
    shared_act = (jax.nn.silu(shared_gu[0]) * shared_gu[1]).astype(jnp.bfloat16)
    shared_part = jnp.dot(shared_act, w_shared_down, preferred_element_type=jnp.float32)
    slot_dest, slot_owner = slot_table(routes, expert_count, capacity)
    slot_source = (slot_owner // top_count).reshape(expert_count, capacity)
    owner_table = slot_owner.reshape(expert_count, capacity)
    padded_two = jnp.concatenate([low_two, jnp.zeros((1, features), jnp.bfloat16)], axis=0)
    arrived = lax.all_to_all(padded_two[slot_source], "ep", split_axis=0, concat_axis=0, tiled=True)
    expert_in = arrived.reshape(-1, features)
    gate_up_weight = w_expert_gu[0]
    down_weight = w_expert_down[0]
    gate_up = jnp.einsum(
        "rd,cdf->crf", expert_in, gate_up_weight, preferred_element_type=jnp.float32
    )
    expert_act = (jax.nn.silu(gate_up[0]) * gate_up[1]).astype(jnp.bfloat16)
    expert_part = jnp.dot(expert_act, down_weight, preferred_element_type=jnp.float32).astype(
        jnp.bfloat16
    )
    expert_part = expert_part.reshape(expert_count, capacity, features)
    returned = lax.all_to_all(expert_part, "ep", split_axis=0, concat_axis=0, tiled=True)
    return_table = returned.reshape(-1, features)
    return_table = jnp.concatenate(
        [return_table, jnp.zeros((1, features), return_table.dtype)], axis=0
    )
    picked = return_table[slot_dest].reshape(seq_rows, top_count, features)
    expert_sum = jnp.zeros((seq_rows, features), jnp.float32)
    for route_slot in range(top_count):
        expert_sum = expert_sum + gate_values[:, route_slot, None] * picked[:, route_slot].astype(
            jnp.float32
        )
    mlp_total = lax.psum(
        (shared_gate[:, None] * shared_part + expert_sum).astype(jnp.bfloat16), "tp"
    ).astype(jnp.float32)
    output = hidden + mlp_total
    output_rows = lax.dynamic_slice_in_dim(output, row_start, out_rows, 0).astype(jnp.bfloat16)
    grad_output = grad_out.astype(jnp.float32)
    grad_sout = (shared_gate[:, None] * grad_output).astype(jnp.bfloat16)
    grad_shared_down = contract(shared_act, grad_sout, 0, 0)
    grad_sgu = gated_backward(contract(grad_sout, w_shared_down, 1, 1), shared_gu)
    grad_shared_gu = jnp.einsum(
        "ld,clf->cdf", low_two, grad_sgu, preferred_element_type=jnp.float32
    )
    grad_low_two = jnp.einsum(
        "clf,cdf->ld", grad_sgu, w_shared_gu, preferred_element_type=jnp.float32
    )
    shared_dot = jnp.sum(grad_output * shared_part, axis=-1)
    gate_dot = jnp.sum(grad_output[:, None, :] * picked.astype(jnp.float32), axis=-1)
    gate_flat = jnp.concatenate([gate_values.reshape(-1), jnp.zeros((1,), jnp.float32)])
    padded_grad = jnp.concatenate([grad_output, jnp.zeros((1, features), jnp.float32)], axis=0)
    sent_grads = (padded_grad[slot_source] * gate_flat[owner_table][:, :, None]).astype(
        jnp.bfloat16
    )
    grad_arrived = lax.all_to_all(sent_grads, "ep", split_axis=0, concat_axis=0, tiled=True)
    grad_arrived = grad_arrived.reshape(-1, features)
    grad_expert_down = contract(expert_act, grad_arrived, 0, 0)
    grad_egu = gated_backward(contract(grad_arrived, down_weight, 1, 1), gate_up)
    grad_expert_gu = jnp.einsum(
        "rd,crf->cdf", expert_in, grad_egu, preferred_element_type=jnp.float32
    )
    grad_sent = jnp.einsum(
        "crf,cdf->rd", grad_egu, gate_up_weight, preferred_element_type=jnp.float32
    ).astype(jnp.bfloat16)
    grad_returned = lax.all_to_all(
        grad_sent.reshape(expert_count, capacity, features),
        "ep",
        split_axis=0,
        concat_axis=0,
        tiled=True,
    )
    grad_pairs = grad_returned.reshape(-1, features)[slot_dest].reshape(
        seq_rows, top_count, features
    )
    grad_low_two = grad_low_two + jnp.sum(grad_pairs.astype(jnp.float32), axis=1)
    grad_low_two, gate_dot, shared_dot = (
        lax.psum(grad_low_two.astype(jnp.bfloat16), "tp").astype(jnp.float32),
        lax.psum(gate_dot.astype(jnp.bfloat16), "tp").astype(jnp.float32),
        lax.psum(shared_dot.astype(jnp.bfloat16), "tp").astype(jnp.float32),
    )
    grad_sgate_logit = (shared_dot * shared_gate * (1.0 - shared_gate)).astype(jnp.bfloat16)
    grad_sgate = contract(low_two, grad_sgate_logit, 0, 0)
    grad_probs = jnp.sum(gate_dot[:, :, None] * route_hits, axis=1)
    grad_logits = router_probs * (
        grad_probs - jnp.sum(router_probs * grad_probs, axis=-1, keepdims=True)
    )
    grad_logits = grad_logits.astype(jnp.bfloat16)
    grad_router = contract(low_two, grad_logits, 0, 0)
    grad_low_two = (
        grad_low_two
        + grad_sgate_logit.astype(jnp.float32)[:, None] * w_sgate.astype(jnp.float32)[None, :]
    )
    grad_low_two = grad_low_two + contract(grad_logits, w_router, 1, 1)
    grad_hidden_norm, grad_norm_two = rms_backward(grad_low_two, norm2_gain, unit_two, scale_two)
    grad_hidden = grad_output + grad_hidden_norm
    grad_attn = grad_hidden.astype(jnp.bfloat16)
    grad_out_weight = contract(attn_mixed, grad_attn, 0, 0)
    grad_mixed = (
        contract(grad_attn, w_out, 1, 1)
        .astype(jnp.bfloat16)
        .reshape(seq_rows, heads_here, head_dim)
    )
    again_probs = jnp.exp(attn_scores() - log_total)
    grad_values = jnp.einsum(
        "hqk,qhd->khd",
        again_probs.astype(jnp.bfloat16),
        grad_mixed,
        preferred_element_type=jnp.float32,
    )
    grad_probs_attn = jnp.einsum(
        "qhd,khd->hqk", grad_mixed, value_rows, preferred_element_type=jnp.float32
    )
    grad_scores = again_probs * (
        grad_probs_attn - jnp.sum(again_probs * grad_probs_attn, axis=-1, keepdims=True)
    )
    grad_scores = grad_scores.astype(jnp.bfloat16)
    grad_queries = (
        jnp.einsum("hqk,khd->qhd", grad_scores, key_rows, preferred_element_type=jnp.float32)
        * score_scale
    )
    grad_keys = (
        jnp.einsum("hqk,qhd->khd", grad_scores, queries, preferred_element_type=jnp.float32)
        * score_scale
    )
    grad_pre = jnp.stack(
        [
            rotate_backward(grad_queries, cosine_table, sine_table),
            rotate_backward(grad_keys, cosine_table, sine_table),
            grad_values,
        ]
    )
    grad_pre = grad_pre.reshape(3, seq_rows, -1).astype(jnp.bfloat16)
    grad_bias = jnp.sum(grad_pre.astype(jnp.float32), axis=1).reshape(3, heads_here, head_dim)
    grad_qkv = jnp.einsum("ld,cle->cde", low_one, grad_pre, preferred_element_type=jnp.float32)
    grad_low_one = lax.psum(
        jnp.einsum("cle,cde->ld", grad_pre, w_qkv, preferred_element_type=jnp.float32).astype(
            jnp.bfloat16
        ),
        "tp",
    ).astype(jnp.float32)
    grad_input_norm, grad_norm_one = rms_backward(grad_low_one, norm1_gain, unit_one, scale_one)
    grad_tokens = lax.dynamic_slice_in_dim(grad_hidden + grad_input_norm, row_start, out_rows, 0)
    summed = (
        lax.psum_scatter(grad_norm_one, "ep", scatter_dimension=0, tiled=True),
        lax.psum_scatter(grad_qkv, "ep", scatter_dimension=1, tiled=True),
        lax.psum_scatter(grad_bias, "ep", scatter_dimension=2, tiled=True),
        lax.psum_scatter(grad_out_weight, "ep", scatter_dimension=1, tiled=True),
        lax.psum_scatter(grad_norm_two, "ep", scatter_dimension=0, tiled=True),
        lax.psum_scatter(grad_router, "ep", scatter_dimension=0, tiled=True),
        lax.psum_scatter(grad_sgate, "ep", scatter_dimension=0, tiled=True),
        lax.psum_scatter(grad_shared_gu, "ep", scatter_dimension=1, tiled=True),
        lax.psum_scatter(grad_shared_down, "ep", scatter_dimension=1, tiled=True),
    )
    return (
        output_rows,
        grad_tokens,
        summed[0],
        summed[1],
        summed[2],
        summed[3],
        summed[4],
        summed[5],
        summed[6],
        summed[7],
        summed[8],
        grad_expert_gu[None],
        grad_expert_down[None],
    )


def solution(mesh):
    return jax.shard_map(
        per_device,
        mesh=mesh,
        in_specs=(
            P("ep", None),
            P(),
            P(None, None, "tp"),
            P(None, "tp", None),
            P("tp", None),
            P(),
            P(),
            P(),
            P(None, None, "tp"),
            P("tp", None),
            P("ep", None, None, "tp"),
            P("ep", "tp", None),
            P("ep", None),
            P("ep", None),
        ),
        out_specs=(
            P(("ep", "tp"), None),
            P(("ep", "tp"), None),
            P("ep"),
            P(None, "ep", "tp"),
            P(None, "tp", "ep"),
            P("tp", "ep"),
            P("ep"),
            P("ep", None),
            P("ep"),
            P(None, "ep", "tp"),
            P("tp", "ep"),
            P("ep", None, None, "tp"),
            P("ep", "tp", None),
        ),
        check_vma=False,
    )
```

profile of v0, /device:TPU:0, one launch (start us, length us, event | category | flops | bytes accessed | tf_op | source)
XLA Modules:
  0.0 1859.8 jit_solution(4364813825440306006)
XLA Ops:
  37.6 21.9 %scatter_custom_fusion = s32[3200]{0:T(1024)S(1)} fusion(s32[2560]{0:T(1024)S(1)} %get-tuple-element.96, s32[2560]{0:T(1024)S(1)} %iota.45, s32[]{:T(128)} %constant.23.clone.1), kind=kCustom, calls=%fused_computation.175 | custom fusion | bytes 12804 | tf_op jit(solution)/shard_map/scatter | solution.py:74
  59.8 164.4 %all-reduce.13.cloned.1.call-done = f32[640,2048]{1,0:T(8,128)} async-done(((f32[640,2048]{1,0:T(8,128)}), f32[640,2048]{1,0:T(8,128)}) %all-reduce.13.cloned.1.call-update) | async-done | bytes 5242896 | tf_op jit(solution)/shard_map/psum | solution.py:134
  234.4 27.7 %gather_fusion = bf16[3200,2048]{1,0:T(8,128)(2,1)} fusion(bf16[641,2048]{1,0:T(8,128)(2,1)} %concatenate.36, s32[4096]{0:T(1024)S(1)} %pad_clamp_fusion.1), kind=kCustom, calls=%fused_computation | custom fusion | bytes 26227200 | tf_op jit(solution)/shard_map/gather | solution.py:153
  262.2 148.5 %all_to_all.20 = bf16[8,400,2048]{2,1,0:T(8,128)(2,1)S(1)} all-to-all(bf16[8,400,2048]{2,1,0:T(8,128)(2,1)} %bitcast.232), channel_id=1, replica_groups=mesh['ep'=8,'tp'=4] {'ep'}, dimensions={0} | all-to-all | bytes 26214400 | tf_op jit(solution)/shard_map/all_to_all | solution.py:153
  450.5 27.3 %gather_fusion.2 = f32[3200,2048]{1,0:T(8,128)} fusion(f32[641,2048]{1,0:T(8,128)} %concatenate.38, s32[4096]{0:T(1024)S(1)} %pad_clamp_fusion.1), kind=kCustom, calls=%fused_computation.2 | custom fusion | bytes 52441600 | tf_op jit(solution)/shard_map/gather | solution.py:195
  512.8 74.1 %all-to-all-done.1 = bf16[8,400,2048]{2,1,0:T(8,128)(2,1)} async-done(((bf16[8,400,2048]{2,1,0:T(8,128)(2,1)}), bf16[8,400,2048]{2,1,0:T(8,128)(2,1)}, u32[]{:S(2)}, u32[]{:S(2)}) %all-to-all-start.1) | async-done | bytes 13107232 | tf_op jit(solution)/shard_map/all_to_all | solution.py:165
  598.3 26.6 %gather_fusion.1 = bf16[2560,2048]{1,0:T(8,128)(2,1)} fusion(bf16[3201,2048]{1,0:T(8,128)(2,1)} %concatenate.37, s32[3072]{0:T(1024)S(1)} %pad_clamp_fusion.3), kind=kCustom, calls=%fused_computation.1 | custom fusion | bytes 20981760 | tf_op jit(solution)/shard_map/gather | solution.py:170
  689.8 147.5 %all_to_all.21 = bf16[8,400,2048]{2,1,0:T(8,128)(2,1)S(1)} all-to-all(bf16[8,400,2048]{2,1,0:T(8,128)(2,1)S(1)} %multiply_convert_fusion), channel_id=1, replica_groups=mesh['ep'=8,'tp'=4] {'ep'}, dimensions={0} | all-to-all | bytes 26214400 | tf_op jit(solution)/shard_map/all_to_all | solution.py:198
  837.3 17.0 fusion.27
  875.1 144.5 %all-to-all-done.3 = bf16[8,400,2048]{2,1,0:T(8,128)(2,1)} async-done(((bf16[8,400,2048]{2,1,0:T(8,128)(2,1)}), bf16[8,400,2048]{2,1,0:T(8,128)(2,1)}, u32[]{:S(2)}, u32[]{:S(2)}) %all-to-all-start.3) | async-done | bytes 13107232 | tf_op jit(solution)/shard_map/all_to_all | solution.py:208
  1019.6 26.8 %gather_fusion.4 = bf16[2560,2048]{1,0:T(8,128)(2,1)} fusion(bf16[3200,2048]{1,0:T(8,128)(2,1)} %bitcast.36, s32[3072]{0:T(1024)S(1)} %pad_clamp_fusion.2), kind=kCustom, calls=%fused_computation.4 | custom fusion | bytes 20981760 | tf_op jit(solution)/shard_map/gather | solution.py:215
  1046.4 19.0 %reshape.317 = f32[640,4,2048]{2,1,0:T(4,128)} reshape(bf16[2560,2048]{1,0:T(8,128)(2,1)} %gather_fusion.4) | data formatting | bytes 31457280 | tf_op jit(solution)/shard_map/convert_element_type | solution.py:218
  1065.4 18.5 reduce_sum.162
  1113.3 31.4 %fusion.69 = (bf16[640,1,2048]{2,1,0:T(2,128)(2,1)S(1)}, bf16[640,1,2048]{2,1,0:T(2,128)(2,1)S(1)}, bf16[640,1,2048]{2,1,0:T(2,128)(2,1)S(1)}, bf16[640,1,2048]{2,1,0:T(2,128)(2,1)S(1)}) fusion(bf16[640,4,2048]{2,1,0:T(4,128)(2,1)} %reshape.304), kind=kLoop, calls=%fused_computation.195 | loop fusion | bytes 20971520 | tf_op jit(solution)/shard_map/slice | solution.py:173
  1144.8 17.1 fusion.4
  1161.9 36.5 %all-reduce.15.cloned.1.call-done = bf16[640,2048]{1,0:T(8,128)(2,1)} async-done(((bf16[640,2048]{1,0:T(8,128)(2,1)}), bf16[640,2048]{1,0:T(8,128)(2,1)}) %all-reduce.15.cloned.1.call-update) | async-done | bytes 2621456 | tf_op jit(solution)/shard_map/psum | solution.py:220
  1314.9 32.4 %reduce-scatter.15.cloned.1.call-done = f32[2,256,1408]{1,2,0:T(8,128)} async-done(((f32[2,2048,1408]{1,2,0:T(8,128)}), f32[2,256,1408]{1,2,0:T(8,128)}) %reduce-scatter.15.cloned.1.call-update) | async-done | bytes 2883600 | tf_op jit(solution)/shard_map/reduce_scatter | solution.py:294
  1350.6 33.6 %reduce-scatter.19.cloned.1.call-done = f32[16,12]{1,0:T(8,128)} async-done(((f32[128,12]{1,0:T(8,128)}), f32[16,12]{1,0:T(8,128)}) %reduce-scatter.19.cloned.1.call-update) | async-done | bytes 784
  1385.7 189.8 %all-reduce.17.cloned.1.call-done = (bf16[640,2048]{1,0:T(8,128)(2,1)}, bf16[640,2048]{1,0:T(8,128)(2,1)}) async-done(((bf16[640,2048]{1,0:T(8,128)(2,1)}, bf16[640,2048]{1,0:T(8,128)(2,1)}), (bf16[640,2048]{1,0:T(8,128)(2,1)}, bf16[640,2048]{1,0:T(8,128)(2,1)})) %all-reduce.17.cloned.1.call-update) | async-done | bytes 5242896 | tf_op jit(solution)/shard_map/psum | solution.py:176
  1582.7 23.8 %all-reduce.6 = (f32[2048]{0:T(1024)S(1)}, f32[2048]{0:T(1024)S(1)}, f32[2048]{0:T(1024)S(1)}) all-reduce(f32[2048]{0:T(1024)S(1)} %get-tuple-element.93, f32[2048]{0:T(1024)S(1)} %copy-done.55, f32[2048]{0:T(1024)S(1)} %bitcast.256), channel_id=2, replica_groups=mesh['ep'=8,'tp'=4] {'ep'}, use_global_device_ids=true, to_apply=%region_26.27.clone | all-reduce | flops 6144 | bytes 49152
  1614.7 55.1 %reduce-scatter.9.cloned.1.call-done = f32[3,256,512]{1,2,0:T(8,128)} async-done(((f32[3,2048,512]{1,2,0:T(8,128)}), f32[3,256,512]{1,2,0:T(8,128)}) %reduce-scatter.9.cloned.1.call-update) | async-done | bytes 1572880 | tf_op jit(solution)/shard_map/reduce_scatter | solution.py:288
  1672.8 87.9 %reduce-scatter.17.cloned.1.call-done = f32[1408,256]{1,0:T(8,128)} async-done(((f32[1408,2048]{1,0:T(8,128)}), f32[1408,256]{1,0:T(8,128)}) %reduce-scatter.17.cloned.1.call-update) | async-done | bytes 1441808 | tf_op jit(solution)/shard_map/reduce_scatter | solution.py:295
  1760.7 37.1 %reduce-scatter.13.cloned.1.call-done = f32[256,8]{0,1:T(8,128)} async-done(((f32[2048,8]{0,1:T(8,128)}), f32[256,8]{0,1:T(8,128)}) %reduce-scatter.13.cloned.1.call-update) | async-done | bytes 8208 | tf_op jit(solution)/shard_map/reduce_scatter | solution.py:292
  1797.8 55.0 %reduce-scatter.11.cloned.1.call-done = f32[512,256]{1,0:T(8,128)} async-done(((f32[512,2048]{1,0:T(8,128)}), f32[512,256]{1,0:T(8,128)}) %reduce-scatter.11.cloned.1.call-update) | async-done | bytes 524304 | tf_op jit(solution)/shard_map/reduce_scatter | solution.py:290
  (303 shorter events, 380.0 us)
Async XLA Ops:
  7.2 403.5 %copy-start = (bf16[1,2,2048,352]{2,3,1,0:T(8,128)(2,1)S(1)}, bf16[1,2,2048,352]{2,3,1,0:T(8,128)(2,1)}, u32[]{:S(2)}) copy-start(bf16[1,2,2048,352]{2,3,1,0:T(8,128)(2,1)} %param.24) | copy-start | bytes 8650756
  7.2 217.0 %all-reduce.13.cloned.1.call-start = ((), (), s32[]{:S(2)}) async-start(), calls=%async_computation.10 | async-start | bytes 10485760 | tf_op jit(solution)/shard_map/psum | solution.py:134
  37.6 21.9 %copy-start.50 = (s32[2560]{0:T(1024)}, s32[2560]{0:T(1024)S(1)}, u32[]{:S(2)}) copy-start(s32[2560]{0:T(1024)S(1)} %get-tuple-element.96) | copy-start | bytes 30724
  59.8 170.8 %copy-start.44 = (f32[2048]{0:T(1024)S(1)}, f32[2048]{0:T(1024)}, u32[]{:S(2)}) copy-start(f32[2048]{0:T(1024)} %param.19) | copy-start | bytes 24580
  436.5 150.4 %all-to-all-start.1 = ((bf16[8,400,2048]{2,1,0:T(8,128)(2,1)}), bf16[8,400,2048]{2,1,0:T(8,128)(2,1)}, u32[]{:S(2)}, u32[]{:S(2)}) async-start(bf16[8,400,2048]{2,1,0:T(8,128)(2,1)} %bitcast.239), calls=%async_computation.1 | async-start | bytes 26214400 | tf_op jit(solution)/shard_map/all_to_all | solution.py:165
  450.5 27.3 %copy-start.52 = (s32[2560]{0:T(1024)S(1)}, s32[2560]{0:T(1024)}, u32[]{:S(2)}) copy-start(s32[2560]{0:T(1024)} %get-tuple-element.95) | copy-start | bytes 30724
  450.5 27.3 %copy-start.34 = (bf16[2048,8]{0,1:T(8,128)(2,1)S(1)}, bf16[2048,8]{0,1:T(8,128)(2,1)}, u32[]{:S(2)}) copy-start(bf16[2048,8]{0,1:T(8,128)(2,1)} %param.20) | copy-start | bytes 98308
  689.7 147.5 %copy-start.65 = (bf16[1,352,2048]{2,1,0:T(8,128)(2,1)S(1)}, bf16[1,352,2048]{2,1,0:T(8,128)(2,1)}, u32[]{:S(2)}) copy-start(bf16[1,352,2048]{2,1,0:T(8,128)(2,1)} %param.25) | copy-start | bytes 4325380
  869.5 150.2 %all-to-all-start.3 = ((bf16[8,400,2048]{2,1,0:T(8,128)(2,1)}), bf16[8,400,2048]{2,1,0:T(8,128)(2,1)}, u32[]{:S(2)}, u32[]{:S(2)}) async-start(bf16[8,400,2048]{2,1,0:T(8,128)(2,1)} %bitcast.240), calls=%async_computation.3 | async-start | bytes 26214400 | tf_op jit(solution)/shard_map/all_to_all | solution.py:208
  875.0 323.4 %all-reduce.15.cloned.1.call-start = ((), (), s32[]{:S(2)}) async-start(), calls=%async_computation.11 | async-start | bytes 5242880 | tf_op jit(solution)/shard_map/psum | solution.py:220
  1097.5 249.8 %reduce-scatter.15.cloned.1.call-start = ((), (), s32[]{:S(2)}) async-start(), calls=%async_computation.15 | async-start | bytes 25952256 | tf_op jit(solution)/shard_map/reduce_scatter | solution.py:294
  1111.9 272.3 %reduce-scatter.19.cloned.1.call-start = ((), (), s32[]{:S(2)}) async-start(), calls=%async_computation.17 | async-start | bytes 73728
  1113.3 31.5 %copy-start.59 = (f32[640]{0:T(1024)S(1)}, f32[640]{0:T(1024)}, u32[]{:S(2)}) copy-start(f32[640]{0:T(1024)} %copy-done.58) | copy-start | bytes 7684
  1144.8 53.7 %copy-start.35 = (bf16[2048,8]{0,1:T(8,128)(2,1)S(1)}, bf16[2048,8]{0,1:T(8,128)(2,1)}, u32[]{:S(2)}) copy-start(bf16[2048,8]{0,1:T(8,128)(2,1)} %param.20) | copy-start | bytes 98308
  1144.8 53.7 %copy-start.45 = (f32[2048]{0:T(1024)S(1)}, f32[2048]{0:T(1024)}, u32[]{:S(2)}) copy-start(f32[2048]{0:T(1024)} %param.19) | copy-start | bytes 24580
  1144.8 53.6 %copy-start.49 = (f32[640]{0:T(1024)S(1)}, f32[640]{0:T(1024)}, u32[]{:S(2)}) copy-start(f32[640]{0:T(1024)} %copy-done.48) | copy-start | bytes 7684
  1198.5 21.3 %slice-start = ((s8[6553600]{0:T(1024)(128)(4,1)}), s8[4194304]{0:T(1024)(128)(4,1)S(1)}, s32[]{:S(2)}) async-start(s8[6553600]{0:T(1024)(128)(4,1)} %bitcast.229), calls=%async_computation.19 | async-start | bytes 8388608
  1249.8 325.7 %all-reduce.17.cloned.1.call-start = ((), (), s32[]{:S(2)}) async-start(), calls=%async_computation.18 | async-start | bytes 10485760 | tf_op jit(solution)/shard_map/psum | solution.py:176
  1258.9 410.9 %reduce-scatter.9.cloned.1.call-start = ((), (), s32[]{:S(2)}) async-start(), calls=%async_computation.12 | async-start | bytes 14155776 | tf_op jit(solution)/shard_map/reduce_scatter | solution.py:288
  1269.9 490.8 %reduce-scatter.17.cloned.1.call-start = ((), (), s32[]{:S(2)}) async-start(), calls=%async_computation.16 | async-start | bytes 12976128 | tf_op jit(solution)/shard_map/reduce_scatter | solution.py:295
  1281.4 516.4 %reduce-scatter.13.cloned.1.call-start = ((), (), s32[]{:S(2)}) async-start(), calls=%async_computation.14 | async-start | bytes 73728 | tf_op jit(solution)/shard_map/reduce_scatter | solution.py:292
  1282.6 570.3 %reduce-scatter.11.cloned.1.call-start = ((), (), s32[]{:S(2)}) async-start(), calls=%async_computation.13 | async-start | bytes 4718592 | tf_op jit(solution)/shard_map/reduce_scatter | solution.py:290
  1314.9 260.6 %copy-start.8 = (bf16[640,2048]{1,0:T(8,128)(2,1)S(1)}, bf16[640,2048]{1,0:T(8,128)(2,1)}, u32[]{:S(2)}) copy-start(bf16[640,2048]{1,0:T(8,128)(2,1)} %param.14) | copy-start | bytes 7864324
  1608.5 244.3 %copy-start.1 = (bf16[1,2,2048,352]{2,3,1,0:T(8,128)(2,1)S(1)}, bf16[1,2,2048,352]{2,3,1,0:T(8,128)(2,1)}, u32[]{:S(2)}) copy-start(bf16[1,2,2048,352]{2,3,1,0:T(8,128)(2,1)} %param.24) | copy-start | bytes 8650756
  (65 other events, 408.3 us)
Sparse Core Ops, SparseCore 0:
  32.5 191.6 all-reduce.12
  1097.6 100.8 all-reduce.14
  1202.1 145.0 reduce-scatter.14
  1350.7 33.5 reduce-scatter.18
  1386.5 188.9 all-reduce.16
  1578.8 90.8 reduce-scatter.8
  1673.8 86.8 reduce-scatter.16
  1764.2 33.5 reduce-scatter.12
  1801.8 51.0 reduce-scatter.10
where the time goes:
time: 1870 us; the launch traced here: 1860 us
  waiting for transfers between devices  911 us (49%)
  blocking collectives  330 us (18%)
  local copies, waits for them, and re-layouts  266 us (14%)
  matrix products  219 us (12%)
  other arithmetic  107 us (6%)
    psum x1, waiting for transfers between devices, per_device(): lax.psum((shared_gate[:, None] * shared_part + expert_sum).astype(jnp.bfl...  190 us
    psum x1, waiting for transfers between devices, per_device(): lax.psum(jnp.dot(attn_mixed, w_out, preferred_element_type=jnp.float32),...  164 us
    all_to_all x1, blocking collectives, per_device(): lax.all_to_all(padded_two[slot_source], 'ep', split_axis=0, concat_axis=0...  149 us
    all_to_all x1, blocking collectives, per_device(): lax.all_to_all(sent_grads, 'ep', split_axis=0, concat_axis=0, tiled=True)  148 us
    all_to_all x1, waiting for transfers between devices, per_device(): lax.all_to_all(grad_sent.reshape(expert_count, capacity, features), 'ep',...  145 us
    reduce_scatter x1, waiting for transfers between devices, per_device(): lax.psum_scatter(grad_shared_down, 'ep', scatter_dimension=1, tiled=True)  87.9 us
    all_to_all x1, waiting for transfers between devices, per_device(): lax.all_to_all(expert_part, 'ep', split_axis=0, concat_axis=0, tiled=True)  74.1 us
    dot_general x9, matrix products, contract(): lax.dot_general(left_side, right_side, (((left_dim,), (right_dim,)), ((),...  70 us
  transfers between devices with their start and end apart: 11, of which 11 were waited for; matrix products, arithmetic and copies ran while one was open for 16% of the time, Pallas kernels for 0%

commit v1 on v0

--- a/solution.py
+++ b/solution.py
@@ -173,8 +173,9 @@
         expert_sum = expert_sum + gate_values[:, route_slot, None] * picked[:, route_slot].astype(
             jnp.float32
         )
-    mlp_total = lax.psum(
-        (shared_gate[:, None] * shared_part + expert_sum).astype(jnp.bfloat16), "tp"
+    mark_the_values = lambda u_in: jax.lax.all_gather(u_in, "tp").sum(axis=0)
+    mlp_total = mark_the_values(
+        (shared_gate[:, None] * shared_part + expert_sum).astype(jnp.bfloat16)
     ).astype(jnp.float32)
     output = hidden + mlp_total
     output_rows = lax.dynamic_slice_in_dim(output, row_start, out_rows, 0).astype(jnp.bfloat16)

time: 1870 us -> 1970 us (1.053)
  waiting for transfers between devices: 911 us -> 1000 us
    all_gather x0 -> x1, waiting for transfers between devices: none -> 182 us  [per_device(): mark_the_values = lambda u_in: jax.lax.all_gather(u_in, 'tp').sum(axis=0)]
    psum x1, waiting for transfers between devices: 190 us -> 105 us  [per_device(): lax.psum(jnp.einsum('cle,cde->ld', grad_pre, w_qkv, preferred_element_typ...]
  transfers between devices with their start and end apart: 11 -> 12, of which waited for: 11 -> 12; matrix products, arithmetic and copies ran while one was open for 16% -> 15% of each run, Pallas kernels for 0% -> 0%
where the time goes in v1:
time: 1970 us; the launch traced here: 1960 us
  waiting for transfers between devices  1000 us (51%)
  blocking collectives  330 us (17%)
  local copies, waits for them, and re-layouts  265 us (13%)
  matrix products  219 us (11%)
  other arithmetic  115 us (6%)
    all_gather x1, waiting for transfers between devices, per_device(): mark_the_values = lambda u_in: jax.lax.all_gather(u_in, 'tp').sum(axis=0)  182 us
    psum x1, waiting for transfers between devices, per_device(): lax.psum(jnp.dot(attn_mixed, w_out, preferred_element_type=jnp.float32),...  164 us
    all_to_all x1, blocking collectives, per_device(): lax.all_to_all(padded_two[slot_source], 'ep', split_axis=0, concat_axis=0...  149 us
    all_to_all x1, blocking collectives, per_device(): lax.all_to_all(sent_grads, 'ep', split_axis=0, concat_axis=0, tiled=True)  148 us
    all_to_all x1, waiting for transfers between devices, per_device(): lax.all_to_all(grad_sent.reshape(expert_count, capacity, features), 'ep',...  145 us
    psum x1, waiting for transfers between devices, per_device(): lax.psum(jnp.einsum('cle,cde->ld', grad_pre, w_qkv, preferred_element_typ...  105 us
    reduce_scatter x1, waiting for transfers between devices, per_device(): lax.psum_scatter(grad_shared_down, 'ep', scatter_dimension=1, tiled=True)  87.9 us
    all_to_all x1, waiting for transfers between devices, per_device(): lax.all_to_all(expert_part, 'ep', split_axis=0, concat_axis=0, tiled=True)  74.1 us
  transfers between devices with their start and end apart: 12, of which 12 were waited for; matrix products, arithmetic and copies ran while one was open for 15% of the time, Pallas kernels for 0%

profile of v1, /device:TPU:0, one launch (start us, length us, event | category | flops | bytes accessed | tf_op | source)
XLA Modules:
  0.0 1958.6 jit_solution(5527026491489622555)
XLA Ops:
  37.6 21.9 %scatter_custom_fusion = s32[3200]{0:T(1024)S(1)} fusion(s32[2560]{0:T(1024)S(1)} %get-tuple-element.96, s32[2560]{0:T(1024)S(1)} %iota.45, s32[]{:T(128)} %constant.24.clone.1), kind=kCustom, calls=%fused_computation.175 | custom fusion | bytes 12804 | tf_op jit(solution)/shard_map/scatter | solution.py:74
  59.8 164.4 %all-reduce.12.cloned.1.call-done = f32[640,2048]{1,0:T(8,128)} async-done(((f32[640,2048]{1,0:T(8,128)}), f32[640,2048]{1,0:T(8,128)}) %all-reduce.12.cloned.1.call-update) | async-done | bytes 5242896 | tf_op jit(solution)/shard_map/psum | solution.py:134
  234.5 27.7 %gather_fusion = bf16[3200,2048]{1,0:T(8,128)(2,1)} fusion(bf16[641,2048]{1,0:T(8,128)(2,1)} %concatenate.36, s32[4096]{0:T(1024)S(1)} %pad_clamp_fusion.1), kind=kCustom, calls=%fused_computation | custom fusion | bytes 26227200 | tf_op jit(solution)/shard_map/gather | solution.py:153
  262.2 148.5 %all_to_all.20 = bf16[8,400,2048]{2,1,0:T(8,128)(2,1)S(1)} all-to-all(bf16[8,400,2048]{2,1,0:T(8,128)(2,1)} %bitcast.233), channel_id=1, replica_groups=mesh['ep'=8,'tp'=4] {'ep'}, dimensions={0} | all-to-all | bytes 26214400 | tf_op jit(solution)/shard_map/all_to_all | solution.py:153
  450.5 27.3 %gather_fusion.2 = f32[3200,2048]{1,0:T(8,128)} fusion(f32[641,2048]{1,0:T(8,128)} %concatenate.38, s32[4096]{0:T(1024)S(1)} %pad_clamp_fusion.1), kind=kCustom, calls=%fused_computation.2 | custom fusion | bytes 52441600 | tf_op jit(solution)/shard_map/gather | solution.py:196
  512.8 74.1 %all-to-all-done.1 = bf16[8,400,2048]{2,1,0:T(8,128)(2,1)} async-done(((bf16[8,400,2048]{2,1,0:T(8,128)(2,1)}), bf16[8,400,2048]{2,1,0:T(8,128)(2,1)}, u32[]{:S(2)}, u32[]{:S(2)}) %all-to-all-start.1) | async-done | bytes 13107232 | tf_op jit(solution)/shard_map/all_to_all | solution.py:165
  598.3 26.6 %gather_fusion.1 = bf16[2560,2048]{1,0:T(8,128)(2,1)} fusion(bf16[3201,2048]{1,0:T(8,128)(2,1)} %concatenate.37, s32[3072]{0:T(1024)S(1)} %pad_clamp_fusion.3), kind=kCustom, calls=%fused_computation.1 | custom fusion | bytes 20981760 | tf_op jit(solution)/shard_map/gather | solution.py:170
  663.2 16.9 gather_fusion.3
  689.8 147.5 %all_to_all.21 = bf16[8,400,2048]{2,1,0:T(8,128)(2,1)S(1)} all-to-all(bf16[8,400,2048]{2,1,0:T(8,128)(2,1)S(1)} %multiply_convert_fusion), channel_id=1, replica_groups=mesh['ep'=8,'tp'=4] {'ep'}, dimensions={0} | all-to-all | bytes 26214400 | tf_op jit(solution)/shard_map/all_to_all | solution.py:199
  875.1 144.5 %all-to-all-done.3 = bf16[8,400,2048]{2,1,0:T(8,128)(2,1)} async-done(((bf16[8,400,2048]{2,1,0:T(8,128)(2,1)}), bf16[8,400,2048]{2,1,0:T(8,128)(2,1)}, u32[]{:S(2)}, u32[]{:S(2)}) %all-to-all-start.3) | async-done | bytes 13107232 | tf_op jit(solution)/shard_map/all_to_all | solution.py:209
  1019.6 26.8 %gather_fusion.4 = bf16[2560,2048]{1,0:T(8,128)(2,1)} fusion(bf16[3200,2048]{1,0:T(8,128)(2,1)} %bitcast.37, s32[3072]{0:T(1024)S(1)} %pad_clamp_fusion.2), kind=kCustom, calls=%fused_computation.4 | custom fusion | bytes 20981760 | tf_op jit(solution)/shard_map/gather | solution.py:216
  1046.4 19.0 reshape.317
  1065.4 18.5 reduce_sum.175
  1112.7 31.4 %fusion.69 = (bf16[640,1,2048]{2,1,0:T(2,128)(2,1)S(1)}, bf16[640,1,2048]{2,1,0:T(2,128)(2,1)S(1)}, bf16[640,1,2048]{2,1,0:T(2,128)(2,1)S(1)}, bf16[640,1,2048]{2,1,0:T(2,128)(2,1)S(1)}) fusion(bf16[640,4,2048]{2,1,0:T(4,128)(2,1)} %reshape.304), kind=kLoop, calls=%fused_computation.195 | loop fusion | bytes 20971520 | tf_op jit(solution)/shard_map/slice | solution.py:173
  1162.1 36.3 %all-reduce.14.cloned.1.call-done = bf16[640,2048]{1,0:T(8,128)(2,1)} async-done(((bf16[640,2048]{1,0:T(8,128)(2,1)}), bf16[640,2048]{1,0:T(8,128)(2,1)}) %all-reduce.14.cloned.1.call-update) | async-done | bytes 2621456 | tf_op jit(solution)/shard_map/psum | solution.py:221
  1314.3 32.9 %reduce-scatter.15.cloned.1.call-done = f32[2,256,1408]{1,2,0:T(8,128)} async-done(((f32[2,2048,1408]{1,2,0:T(8,128)}), f32[2,256,1408]{1,2,0:T(8,128)}) %reduce-scatter.15.cloned.1.call-update) | async-done | bytes 2883600 | tf_op jit(solution)/shard_map/reduce_scatter | solution.py:295
  1350.6 182.0 %all-gather.3.cloned.1.call-done = bf16[2560,2048]{1,0:T(8,128)(2,1)} async-done(((bf16[640,2048]{1,0:T(8,128)(2,1)}), bf16[2560,2048]{1,0:T(8,128)(2,1)}) %all-gather.3.cloned.1.call-update) | async-done | bytes 10485776 | tf_op jit(solution)/shard_map/all_gather | solution.py:176
  1542.2 25.5 %reduce-scatter.19.cloned.1.call-done = f32[16,12]{1,0:T(8,128)} async-done(((f32[128,12]{1,0:T(8,128)}), f32[16,12]{1,0:T(8,128)}) %reduce-scatter.19.cloned.1.call-update) | async-done | bytes 784
  1569.2 104.9 %all-reduce.16.cloned.1.call-done = bf16[640,2048]{1,0:T(8,128)(2,1)} async-done(((bf16[640,2048]{1,0:T(8,128)(2,1)}), bf16[640,2048]{1,0:T(8,128)(2,1)}) %all-reduce.16.cloned.1.call-update) | async-done | bytes 2621456 | tf_op jit(solution)/shard_map/psum | solution.py:279
  1682.4 23.8 %all-reduce.6 = (f32[2048]{0:T(1024)S(1)}, f32[2048]{0:T(1024)S(1)}, f32[2048]{0:T(1024)S(1)}) all-reduce(f32[2048]{0:T(1024)S(1)} %get-tuple-element.93, f32[2048]{0:T(1024)S(1)} %copy-done.54, f32[2048]{0:T(1024)S(1)} %bitcast.258), channel_id=3, replica_groups=mesh['ep'=8,'tp'=4] {'ep'}, use_global_device_ids=true, to_apply=%region_26.27.clone | all-reduce | flops 6144 | bytes 49152
  1711.7 56.9 %reduce-scatter.9.cloned.1.call-done = f32[3,256,512]{1,2,0:T(8,128)} async-done(((f32[3,2048,512]{1,2,0:T(8,128)}), f32[3,256,512]{1,2,0:T(8,128)}) %reduce-scatter.9.cloned.1.call-update) | async-done | bytes 1572880 | tf_op jit(solution)/shard_map/reduce_scatter | solution.py:289
  1771.6 87.9 %reduce-scatter.17.cloned.1.call-done = f32[1408,256]{1,0:T(8,128)} async-done(((f32[1408,2048]{1,0:T(8,128)}), f32[1408,256]{1,0:T(8,128)}) %reduce-scatter.17.cloned.1.call-update) | async-done | bytes 1441808 | tf_op jit(solution)/shard_map/reduce_scatter | solution.py:296
  1859.5 37.1 %reduce-scatter.13.cloned.1.call-done = f32[256,8]{0,1:T(8,128)} async-done(((f32[2048,8]{0,1:T(8,128)}), f32[256,8]{0,1:T(8,128)}) %reduce-scatter.13.cloned.1.call-update) | async-done | bytes 8208 | tf_op jit(solution)/shard_map/reduce_scatter | solution.py:293
  1896.6 54.9 %reduce-scatter.11.cloned.1.call-done = f32[512,256]{1,0:T(8,128)} async-done(((f32[512,2048]{1,0:T(8,128)}), f32[512,256]{1,0:T(8,128)}) %reduce-scatter.11.cloned.1.call-update) | async-done | bytes 524304 | tf_op jit(solution)/shard_map/reduce_scatter | solution.py:291
  (309 shorter events, 404.7 us)
Async XLA Ops:
  7.2 403.6 %copy-start = (bf16[1,2,2048,352]{2,3,1,0:T(8,128)(2,1)S(1)}, bf16[1,2,2048,352]{2,3,1,0:T(8,128)(2,1)}, u32[]{:S(2)}) copy-start(bf16[1,2,2048,352]{2,3,1,0:T(8,128)(2,1)} %param.24) | copy-start | bytes 8650756
  7.2 216.9 %all-reduce.12.cloned.1.call-start = ((), (), s32[]{:S(2)}) async-start(), calls=%async_computation.10 | async-start | bytes 10485760 | tf_op jit(solution)/shard_map/psum | solution.py:134
  59.8 170.9 %copy-start.43 = (f32[2048]{0:T(1024)S(1)}, f32[2048]{0:T(1024)}, u32[]{:S(2)}) copy-start(f32[2048]{0:T(1024)} %param.19) | copy-start | bytes 24580
  436.5 150.4 %all-to-all-start.1 = ((bf16[8,400,2048]{2,1,0:T(8,128)(2,1)}), bf16[8,400,2048]{2,1,0:T(8,128)(2,1)}, u32[]{:S(2)}, u32[]{:S(2)}) async-start(bf16[8,400,2048]{2,1,0:T(8,128)(2,1)} %bitcast.240), calls=%async_computation.1 | async-start | bytes 26214400 | tf_op jit(solution)/shard_map/all_to_all | solution.py:165
  450.5 27.3 %copy-start.51 = (s32[2560]{0:T(1024)S(1)}, s32[2560]{0:T(1024)}, u32[]{:S(2)}) copy-start(s32[2560]{0:T(1024)} %get-tuple-element.95) | copy-start | bytes 30724
  450.5 27.3 %copy-start.33 = (bf16[2048,8]{0,1:T(8,128)(2,1)S(1)}, bf16[2048,8]{0,1:T(8,128)(2,1)}, u32[]{:S(2)}) copy-start(bf16[2048,8]{0,1:T(8,128)(2,1)} %param.20) | copy-start | bytes 98308
  689.8 147.5 %copy-start.66 = (bf16[1,352,2048]{2,1,0:T(8,128)(2,1)S(1)}, bf16[1,352,2048]{2,1,0:T(8,128)(2,1)}, u32[]{:S(2)}) copy-start(bf16[1,352,2048]{2,1,0:T(8,128)(2,1)} %param.25) | copy-start | bytes 4325380
  869.4 150.1 %all-to-all-start.3 = ((bf16[8,400,2048]{2,1,0:T(8,128)(2,1)}), bf16[8,400,2048]{2,1,0:T(8,128)(2,1)}, u32[]{:S(2)}, u32[]{:S(2)}) async-start(bf16[8,400,2048]{2,1,0:T(8,128)(2,1)} %bitcast.241), calls=%async_computation.3 | async-start | bytes 26214400 | tf_op jit(solution)/shard_map/all_to_all | solution.py:209
  875.0 323.5 %all-reduce.14.cloned.1.call-start = ((), (), s32[]{:S(2)}) async-start(), calls=%async_computation.11 | async-start | bytes 5242880 | tf_op jit(solution)/shard_map/psum | solution.py:221
  1097.4 249.8 %reduce-scatter.15.cloned.1.call-start = ((), (), s32[]{:S(2)}) async-start(), calls=%async_computation.16 | async-start | bytes 25952256 | tf_op jit(solution)/shard_map/reduce_scatter | solution.py:295
  1111.9 420.6 %all-gather.3.cloned.1.call-start = ((), (), s32[]{:S(2)}) async-start(), calls=%async_computation.18 | async-start | bytes 13107200 | tf_op jit(solution)/shard_map/all_gather | solution.py:176
  1112.7 31.5 %copy-start.58 = (f32[640]{0:T(1024)S(1)}, f32[640]{0:T(1024)}, u32[]{:S(2)}) copy-start(f32[640]{0:T(1024)} %copy-done.57) | copy-start | bytes 7684
  1144.2 54.2 %copy-start.34 = (bf16[2048,8]{0,1:T(8,128)(2,1)S(1)}, bf16[2048,8]{0,1:T(8,128)(2,1)}, u32[]{:S(2)}) copy-start(bf16[2048,8]{0,1:T(8,128)(2,1)} %param.20) | copy-start | bytes 98308
  1144.2 54.2 %copy-start.44 = (f32[2048]{0:T(1024)S(1)}, f32[2048]{0:T(1024)}, u32[]{:S(2)}) copy-start(f32[2048]{0:T(1024)} %param.19) | copy-start | bytes 24580
  1144.2 54.2 %copy-start.48 = (f32[640]{0:T(1024)S(1)}, f32[640]{0:T(1024)}, u32[]{:S(2)}) copy-start(f32[640]{0:T(1024)} %copy-done.47) | copy-start | bytes 7684
  1161.2 406.5 %reduce-scatter.19.cloned.1.call-start = ((), (), s32[]{:S(2)}) async-start(), calls=%async_computation.19 | async-start | bytes 73728
  1249.8 424.3 %all-reduce.16.cloned.1.call-start = ((), (), s32[]{:S(2)}) async-start(), calls=%async_computation.12 | async-start | bytes 5242880 | tf_op jit(solution)/shard_map/psum | solution.py:279
  1258.8 509.8 %reduce-scatter.9.cloned.1.call-start = ((), (), s32[]{:S(2)}) async-start(), calls=%async_computation.13 | async-start | bytes 14155776 | tf_op jit(solution)/shard_map/reduce_scatter | solution.py:289
  1269.1 590.4 %reduce-scatter.17.cloned.1.call-start = ((), (), s32[]{:S(2)}) async-start(), calls=%async_computation.17 | async-start | bytes 12976128 | tf_op jit(solution)/shard_map/reduce_scatter | solution.py:296
  1281.2 615.5 %reduce-scatter.13.cloned.1.call-start = ((), (), s32[]{:S(2)}) async-start(), calls=%async_computation.15 | async-start | bytes 73728 | tf_op jit(solution)/shard_map/reduce_scatter | solution.py:293
  1282.4 669.2 %reduce-scatter.11.cloned.1.call-start = ((), (), s32[]{:S(2)}) async-start(), calls=%async_computation.14 | async-start | bytes 4718592 | tf_op jit(solution)/shard_map/reduce_scatter | solution.py:291
  1532.5 141.5 %copy-start.63 = (f32[2048]{0:T(1024)S(1)}, f32[2048]{0:T(1024)}, u32[]{:S(2)}) copy-start(f32[2048]{0:T(1024)} %param.15) | copy-start | bytes 24580
  1569.2 113.2 %copy-start.54 = (f32[2048]{0:T(1024)S(1)}, f32[2048]{0:T(1024)}, u32[]{:S(2)}) copy-start(f32[2048]{0:T(1024)} %get-tuple-element.91) | copy-start | bytes 24580
  1674.1 277.5 %copy-start.1 = (bf16[1,2,2048,352]{2,3,1,0:T(8,128)(2,1)S(1)}, bf16[1,2,2048,352]{2,3,1,0:T(8,128)(2,1)}, u32[]{:S(2)}) copy-start(bf16[1,2,2048,352]{2,3,1,0:T(8,128)(2,1)} %param.24) | copy-start | bytes 8650756
  (67 other events, 577.2 us)
Sparse Core Ops, SparseCore 0:
  32.5 191.6 all-reduce.11
  1097.5 100.8 all-reduce.13
  1202.1 145.0 reduce-scatter.14
  1348.6 183.8 all-gather.2
  1536.0 31.6 reduce-scatter.18
  1569.9 104.0 all-reduce.15
  1677.6 90.9 reduce-scatter.8
  1772.6 86.8 reduce-scatter.16
  1863.1 33.5 reduce-scatter.12
  1900.4 51.0 reduce-scatter.10
